TPU v7x, 16 devices: a 4x2x1 block of a 4x4x8 slice. The times are simulated.
16 devices in a mesh: dp: 2 (over y, z), sp: 8 (over x, core).
Axes of the slice: x: 4, y: 2, z: 1, core: 2. Of those that a mesh axis runs over, the one named last changes fastest.
The devices are a block of a 4x4x8 slice.
Arguments:
- latent: bfloat16 [24, 64, 16, 640], P('dp', 'sp'), parts along dimension 0
- context: bfloat16 [24, 77, 2048], P('dp'), parts along dimension 0
- gn_gain: bfloat16 [640], replicated
- gn_bias: bfloat16 [640], replicated
- w_in: bfloat16 [640, 640], replicated
- b_in: bfloat16 [640], replicated
- ln_gain: bfloat16 [2, 3, 640], replicated
- ln_bias: bfloat16 [2, 3, 640], replicated
- w_self: bfloat16 [2, 4, 640, 640], replicated
- b_self: bfloat16 [2, 640], replicated
- w_cross_q: bfloat16 [2, 640, 640], replicated
- w_cross_kv: bfloat16 [2, 2, 2048, 640], replicated
- w_cross_o: bfloat16 [2, 640, 640], replicated
- b_cross: bfloat16 [2, 640], replicated
- w_ff1: bfloat16 [2, 640, 5120], replicated
- b_ff1: bfloat16 [2, 5120], replicated
- w_ff2: bfloat16 [2, 2560, 640], replicated
- b_ff2: bfloat16 [2, 640], replicated
- w_out: bfloat16 [640, 640], replicated
- b_out: bfloat16 [640], replicated
Outputs:
- output: bfloat16 [24, 64, 16, 640], P('dp', 'sp'), parts along dimension 0
There are 2 independent parts. A program takes and returns all parts, laid end to end along the dimension named above; an argument that names none is the same for every part.
All inputs are finite; a program needn't handle non-finite values.
Results may differ from a plain program's by a relative error of at most 0.0130236.
Values are sent between devices in bfloat16 or wider.
A program may use at most 768 MiB of HBM per device.

v0:
```python
import jax
import jax.numpy as jnp
from jax import lax
from jax.sharding import PartitionSpec as P

HEAD_DIM = 64
NUM_GROUPS = 32


def layer_norm(hidden, gain, bias):
    vals = hidden.astype(jnp.float32)
    mean_val = jnp.mean(vals, axis=-1, keepdims=True)
    centered = vals - mean_val
    var_val = jnp.mean(centered * centered, axis=-1, keepdims=True)
    scaled = centered * lax.rsqrt(var_val + 1e-5)
    return (scaled * gain.astype(jnp.float32) + bias.astype(jnp.float32)).astype(jnp.bfloat16)


def project(act, weight):
    return jnp.einsum('btc,cd->btd', act, weight, preferred_element_type=jnp.float32)


def attend(query, keys, values):
    batch, q_len, channels = query.shape
    k_len = keys.shape[1]
    heads = channels // HEAD_DIM
    q_heads = query.reshape(batch, q_len, heads, HEAD_DIM)
    k_heads = keys.reshape(batch, k_len, heads, HEAD_DIM)
    v_heads = values.reshape(batch, k_len, heads, HEAD_DIM)
    scores = jnp.einsum('bqhd,bkhd->bhqk', q_heads, k_heads, preferred_element_type=jnp.float32) * (HEAD_DIM ** -0.5)
    attn_prob = jax.nn.softmax(scores, axis=-1).astype(jnp.bfloat16)
    head_out = jnp.einsum('bhqk,bkhd->bqhd', attn_prob, v_heads, preferred_element_type=jnp.float32)
    return head_out.astype(jnp.bfloat16).reshape(batch, q_len, channels)


def solution(mesh):
    seq_devices = mesh.shape['sp']
    tok_spec = P('dp', 'sp', None, None)
    ctx_spec = P('dp', None, None)
    replicated = P()

    def local_forward(latent, context, gn_gain, gn_bias, w_in, b_in, ln_gain, ln_bias, w_self, b_self, w_cross_q, w_cross_kv, w_cross_o, b_cross, w_ff1, b_ff1, w_ff2, b_ff2, w_out, b_out):
        batch, rows, columns, channels = latent.shape
        tokens = rows * columns
        group_ch = channels // NUM_GROUPS
        ff_dim = w_ff2.shape[1]
        lat_f32 = latent.astype(jnp.float32).reshape(batch, tokens, NUM_GROUPS, group_ch)
        part_sums = jnp.stack([jnp.sum(lat_f32, axis=(1, 3)), jnp.sum(lat_f32 * lat_f32, axis=(1, 3))], axis=1)
        full_sums = lax.psum(part_sums, 'sp')
        elem_count = float(tokens * seq_devices * group_ch)
        grp_mean = full_sums[:, 0] / elem_count
        grp_var = jnp.maximum(full_sums[:, 1] / elem_count - grp_mean * grp_mean, 0.0)
        inv_std = lax.rsqrt(grp_var + 1e-6)
        normed = ((lat_f32 - grp_mean[:, None, :, None]) * inv_std[:, None, :, None]).reshape(batch, tokens, channels)
        normed = (normed * gn_gain.astype(jnp.float32) + gn_bias.astype(jnp.float32)).astype(jnp.bfloat16)
        hidden = (project(normed, w_in) + b_in.astype(jnp.float32)).astype(jnp.bfloat16)
        for layer_idx in range(w_self.shape[0]):
            normed = layer_norm(hidden, ln_gain[layer_idx, 0], ln_bias[layer_idx, 0])
            query = project(normed, w_self[layer_idx, 0]).astype(jnp.bfloat16)
            kv_local = jnp.einsum('btc,jcd->jbtd', normed, w_self[layer_idx, 1:3], preferred_element_type=jnp.float32).astype(jnp.bfloat16)
            kv_all = lax.all_gather(kv_local, 'sp', axis=2, tiled=True)
            attn_out = attend(query, kv_all[0], kv_all[1])
            hidden = (hidden.astype(jnp.float32) + project(attn_out, w_self[layer_idx, 3]) + b_self[layer_idx].astype(jnp.float32)).astype(jnp.bfloat16)
            normed = layer_norm(hidden, ln_gain[layer_idx, 1], ln_bias[layer_idx, 1])
            query = project(normed, w_cross_q[layer_idx]).astype(jnp.bfloat16)
            text_kv = jnp.einsum('blc,jcd->jbld', context, w_cross_kv[layer_idx], preferred_element_type=jnp.float32).astype(jnp.bfloat16)
            attn_out = attend(query, text_kv[0], text_kv[1])
            hidden = (hidden.astype(jnp.float32) + project(attn_out, w_cross_o[layer_idx]) + b_cross[layer_idx].astype(jnp.float32)).astype(jnp.bfloat16)
            normed = layer_norm(hidden, ln_gain[layer_idx, 2], ln_bias[layer_idx, 2])
            ff_proj = (project(normed, w_ff1[layer_idx]) + b_ff1[layer_idx].astype(jnp.float32)).astype(jnp.bfloat16)
            gated = (ff_proj[..., :ff_dim].astype(jnp.float32) * jax.nn.gelu(ff_proj[..., ff_dim:].astype(jnp.float32), approximate=False)).astype(jnp.bfloat16)
            hidden = (hidden.astype(jnp.float32) + project(gated, w_ff2[layer_idx]) + b_ff2[layer_idx].astype(jnp.float32)).astype(jnp.bfloat16)
        result = project(hidden, w_out) + b_out.astype(jnp.float32) + latent.reshape(batch, tokens, channels).astype(jnp.float32)
        return result.astype(jnp.bfloat16).reshape(batch, rows, columns, channels)

    in_specs = (tok_spec, ctx_spec) + (replicated,) * 18
    return jax.shard_map(local_forward, mesh=mesh, in_specs=in_specs, out_specs=tok_spec, check_vma=False)
```

profile of v0, /device:TPU:113, one launch (start us, length us, event | category | flops | bytes accessed | tf_op | source)
XLA Modules:
  0.0 767.1 jit_solution(9657203907290566393)
XLA Ops:
  9.6 24.0 %psum.7 = f32[12,2,32]{2,0,1:T(8,128)S(1)} all-reduce(f32[12,2,32]{2,0,1:T(8,128)S(1)} %pad_maximum_fusion), channel_id=1, replica_groups=mesh['dp'=2,'sp'=8] {'sp'}, use_global_device_ids=true, to_apply=%region_4.0 | all-reduce | flops 768 | bytes 6144 | tf_op jit(solution)/shard_map/psum | solution.py:49
  38.6 6.5 convert_bitcast_fusion.1
  45.4 4.5 convolution_convert_fusion.1
  49.9 3.9 copy.38
  53.9 8.6 %convert_bitcast_fusion.3 = bf16[2,12,77,640]{3,2,1,0:T(8,128)(2,1)S(1)} fusion(bf16[12,77,2048]{2,1,0:T(8,128)(2,1)} %param.21, bf16[2,2,2048,640]{3,2,1,0:T(8,128)(2,1)} %param.31), kind=kOutput, calls=%fused_computation.198 | convolution fusion | flops 4845603840 | bytes 11540480 | tf_op jit(solution)/shard_map/blc,jcd->jbld/dot_general | solution.py:66
  69.9 121.8 %all-gather.3.cloned.1.call-done = bf16[2,12,1024,640]{3,2,0,1:T(8,128)(2,1)} async-done(((bf16[2,12,128,640]{3,2,0,1:T(8,128)(2,1)}), bf16[2,12,1024,640]{3,2,0,1:T(8,128)(2,1)}) %all-gather.3.cloned.1.call-update) | async-done | bytes 31457296 | tf_op jit(solution)/shard_map/all_gather | solution.py:61
  191.7 21.9 %fusion.353 = (bf16[1,12,1024,640]{3,2,0,1:T(8,128)(2,1)}, bf16[1,12,1024,640]{3,2,0,1:T(8,128)(2,1)}) fusion(bf16[2,12,1024,640]{3,2,0,1:T(8,128)(2,1)} %all-gather.3.cloned.1.call-done), kind=kLoop, calls=%fused_computation.360 | loop fusion | bytes 62914560 | tf_op jit(solution)/shard_map/slice | solution.py:62
  213.6 20.7 %copy.39 = bf16[1,12,1024,640]{2,3,1,0:T(8,128)(2,1)} copy(bf16[1,12,1024,640]{3,2,0,1:T(8,128)(2,1)} %get-tuple-element.27) | data formatting | bytes 31457280 | tf_op jit(solution)/shard_map/slice | solution.py:62
  234.3 20.8 %copy.37 = bf16[1,12,1024,640]{2,3,1,0:T(8,128)(2,1)} copy(bf16[1,12,1024,640]{3,2,0,1:T(8,128)(2,1)} %get-tuple-element.28) | data formatting | bytes 31457280 | tf_op jit(solution)/shard_map/slice | solution.py:62
  255.1 30.4 %fusion.356 = (f32[12,10,128]{2,1,0:T(8,128)S(1)}, f32[12,10,128,1024]{3,2,1,0:T(8,128)}) fusion(bf16[12,128,10,64]{1,3,2,0:T(8,128)(2,1)S(1)} %bitcast.222, bf16[12,1024,10,64]{1,3,2,0:T(8,128)(2,1)} %bitcast.214), kind=kOutput, calls=%fused_computation.363 | convolution fusion | flops 2060452864 | bytes 80670720 | tf_op jit(solution)/shard_map/sub | solution.py:31
  285.4 28.3 %fusion.201 = bf16[12,10,64,128]{3,2,1,0:T(8,128)(2,1)} fusion(bf16[12,1024,10,64]{1,3,2,0:T(8,128)(2,1)} %bitcast.215, f32[12,10,128,1024]{3,2,1,0:T(8,128)} %get-tuple-element.38, f32[12,10,128]{2,1,0:T(8,128)S(1)} %get-tuple-element.37), kind=kOutput, calls=%fused_computation.223 | convolution fusion | flops 2045706240 | bytes 80670720 | tf_op jit(solution)/shard_map/bhqk,bkhd->bqhd/dot_general | solution.py:32
  313.7 4.1 convert_reduce_fusion.4
  324.5 6.4 fusion.357
  330.8 3.3 fusion.209
  337.4 18.4 %add_convert_fusion.1 = bf16[12,128,5120]{2,1,0:T(8,128)(2,1)} fusion(f32[5120]{0:T(1024)S(1)} %bitcast.229, bf16[2,640,5120]{2,1,0:T(8,128)(2,1)} %param.34, bf16[12,128,640]{2,1,0:T(8,128)(2,1)S(1)} %get-tuple-element.44, f32[640]{0:T(1024)S(1)} %copy-done.28, f32[640]{0:T(1024)S(1)} %copy-done.29, f32[12,128]{1,0:T(8,128)S(1)} %add_rsqrt_fusion.3, ...), kind=kOutput, calls=%fused_computation.13 | convolution fusion | flops 10087956480 | bytes 24286208 | tf_op jit(solution)/shard_map/btc,cd->btd/dot_general | solution.py:20
  355.8 42.2 %convert_reduce_fusion.2 = (f32[12,128]{1,0:T(8,128)S(1)}, bf16[12,128,640]{2,1,0:T(8,128)(2,1)S(1)}) fusion(f32[640]{0:T(1024)S(1)} %copy-done.36, bf16[2,2560,640]{2,1,0:T(8,128)(2,1)} %param.36, bf16[12,128,5120]{2,1,0:T(8,128)(2,1)} %add_convert_fusion.1, bf16[12,128,640]{2,1,0:T(8,128)(2,1)S(1)} %get-tuple-element.44), kind=kOutput, calls=%fused_computation.102 | convolution fusion | flops 5306448384 | bytes 22946304 | tf_op jit(solution)/shard_map/btc,cd->btd/dot_general | solution.py:20
  399.4 6.6 convert_bitcast_fusion
  406.0 8.6 %convert_bitcast_fusion.2 = bf16[2,12,77,640]{3,2,1,0:T(8,128)(2,1)S(1)} fusion(bf16[12,77,2048]{2,1,0:T(8,128)(2,1)} %param.21, bf16[2,2,2048,640]{3,2,1,0:T(8,128)(2,1)} %param.31), kind=kOutput, calls=%fused_computation.195 | convolution fusion | flops 4845603840 | bytes 11540480 | tf_op jit(solution)/shard_map/blc,jcd->jbld/dot_general | solution.py:66
  420.1 5.2 convolution_convert_fusion
  425.3 2.8 copy.46
  428.1 122.6 %all-gather.5.cloned.1.call-done = bf16[2,12,1024,640]{3,2,0,1:T(8,128)(2,1)} async-done(((bf16[2,12,128,640]{3,2,0,1:T(8,128)(2,1)}), bf16[2,12,1024,640]{3,2,0,1:T(8,128)(2,1)}) %all-gather.5.cloned.1.call-update) | async-done | bytes 31457296 | tf_op jit(solution)/shard_map/all_gather | solution.py:61
  550.8 21.9 %fusion.352 = (bf16[1,12,1024,640]{3,2,0,1:T(8,128)(2,1)}, bf16[1,12,1024,640]{3,2,0,1:T(8,128)(2,1)}) fusion(bf16[2,12,1024,640]{3,2,0,1:T(8,128)(2,1)} %all-gather.5.cloned.1.call-done), kind=kLoop, calls=%fused_computation.359 | loop fusion | bytes 62914560 | tf_op jit(solution)/shard_map/slice | solution.py:62
  572.7 20.7 %copy.47 = bf16[1,12,1024,640]{2,3,1,0:T(8,128)(2,1)} copy(bf16[1,12,1024,640]{3,2,0,1:T(8,128)(2,1)} %get-tuple-element.25) | data formatting | bytes 31457280 | tf_op jit(solution)/shard_map/slice | solution.py:62
  593.3 20.7 %copy.45 = bf16[1,12,1024,640]{2,3,1,0:T(8,128)(2,1)} copy(bf16[1,12,1024,640]{3,2,0,1:T(8,128)(2,1)} %get-tuple-element.26) | data formatting | bytes 31457280 | tf_op jit(solution)/shard_map/slice | solution.py:62
  614.0 30.8 %fusion.358 = (f32[12,10,128]{2,1,0:T(8,128)S(1)}, f32[12,10,128,1024]{3,2,1,0:T(8,128)}) fusion(bf16[12,128,10,64]{1,3,2,0:T(8,128)(2,1)S(1)} %bitcast.223, bf16[12,1024,10,64]{1,3,2,0:T(8,128)(2,1)} %bitcast.216), kind=kOutput, calls=%fused_computation.365 | convolution fusion | flops 2060452864 | bytes 80670720 | tf_op jit(solution)/shard_map/sub | solution.py:31
  644.8 28.1 %fusion.200 = bf16[12,10,64,128]{3,2,1,0:T(8,128)(2,1)} fusion(bf16[12,1024,10,64]{1,3,2,0:T(8,128)(2,1)} %bitcast.217, f32[12,10,128,1024]{3,2,1,0:T(8,128)} %get-tuple-element.48, f32[12,10,128]{2,1,0:T(8,128)S(1)} %get-tuple-element.47), kind=kOutput, calls=%fused_computation.222 | convolution fusion | flops 2045706240 | bytes 80670720 | tf_op jit(solution)/shard_map/bhqk,bkhd->bqhd/dot_general | solution.py:32
  672.9 4.1 convert_reduce_fusion.1
  683.4 6.4 fusion.359
  689.8 3.3 fusion.208
  696.4 18.4 %add_convert_fusion = bf16[12,128,5120]{2,1,0:T(8,128)(2,1)} fusion(f32[5120]{0:T(1024)S(1)} %bitcast.228, bf16[2,640,5120]{2,1,0:T(8,128)(2,1)} %param.34, bf16[12,128,640]{2,1,0:T(8,128)(2,1)S(1)} %get-tuple-element.54, f32[640]{0:T(1024)S(1)} %copy-done.22, f32[640]{0:T(1024)S(1)} %copy-done.23, f32[12,128]{1,0:T(8,128)S(1)} %add_rsqrt_fusion, ...), kind=kOutput, calls=%fused_computation.12 | convolution fusion | flops 10087956480 | bytes 24286208 | tf_op jit(solution)/shard_map/btc,cd->btd/dot_general | solution.py:20
  714.8 41.9 %fusion.394 = bf16[12,128,640]{2,1,0:T(8,128)(2,1)S(1)} fusion(bf16[12,128,640]{2,1,0:T(8,128)(2,1)S(1)} %get-tuple-element.54, f32[640]{0:T(1024)S(1)} %copy-done.33, bf16[2,2560,640]{2,1,0:T(8,128)(2,1)} %param.36, bf16[12,128,5120]{2,1,0:T(8,128)(2,1)} %add_convert_fusion), kind=kOutput, calls=%fused_computation.175.clone.clone.1 | convolution fusion | flops 5304483840 | bytes 22940160 | tf_op jit(solution)/shard_map/btc,cd->btd/dot_general | solution.py:20
  756.7 3.3 fusion.153
  (149 shorter events, 41.7 us)
Async XLA Ops:
  6.5 28.5 %copy-start = (bf16[640,640]{1,0:T(8,128)(2,1)S(1)}, bf16[640,640]{1,0:T(8,128)(2,1)}, u32[]{:S(2)}) copy-start(bf16[640,640]{1,0:T(8,128)(2,1)} %param.24) | copy-start | bytes 2457604
  6.6 27.7 %copy-start.2 = (bf16[12,8,16,640]{3,2,1,0:T(8,128)(2,1)S(1)}, bf16[12,8,16,640]{3,2,1,0:T(8,128)(2,1)}, u32[]{:S(2)}) copy-start(bf16[12,8,16,640]{3,2,1,0:T(8,128)(2,1)} %param.20) | copy-start | bytes 5898244
  6.6 27.7 %copy-start.37 = (bf16[640]{0:T(1024)(128)(2,1)S(1)}, bf16[640]{0:T(1024)(128)(2,1)}, u32[]{:S(2)}) copy-start(bf16[640]{0:T(1024)(128)(2,1)} %param.22) | copy-start | bytes 3844
  6.6 27.7 %copy-start.38 = (bf16[640]{0:T(1024)(128)(2,1)S(1)}, bf16[640]{0:T(1024)(128)(2,1)}, u32[]{:S(2)}) copy-start(bf16[640]{0:T(1024)(128)(2,1)} %param.23) | copy-start | bytes 3844
  6.6 27.7 %copy-start.39 = (bf16[640]{0:T(1024)(128)(2,1)S(1)}, bf16[640]{0:T(1024)(128)(2,1)}, u32[]{:S(2)}) copy-start(bf16[640]{0:T(1024)(128)(2,1)} %param.25) | copy-start | bytes 3844
  6.6 185.1 %all-gather.3.cloned.1.call-start = ((), (), s32[]{:S(2)}) async-start(), calls=%async_computation | async-start | bytes 35389440 | tf_op jit(solution)/shard_map/all_gather | solution.py:61
  37.1 8.3 %copy-start.4 = (bf16[12,128,640]{2,1,0:T(8,128)(2,1)}, bf16[12,128,640]{2,1,0:T(8,128)(2,1)S(1)}, u32[]{:S(2)}) copy-start(bf16[12,128,640]{2,1,0:T(8,128)(2,1)S(1)} %get-tuple-element.36) | copy-start | bytes 5898244
  45.2 505.6 %all-gather.5.cloned.1.call-start = ((), (), s32[]{:S(2)}) async-start(), calls=%async_computation.1 | async-start | bytes 35389440 | tf_op jit(solution)/shard_map/all_gather | solution.py:61
  62.7 4.8 copy-start.19
  62.7 5.4 copy-start.20
  62.7 5.9 copy-start.21
  62.7 6.5 copy-start.15
  234.3 20.8 %copy-start.10 = (bf16[12,128,640]{1,2,0:T(8,128)(2,1)S(1)}, bf16[12,128,640]{1,2,0:T(8,128)(2,1)}, u32[]{:S(2)}) copy-start(bf16[12,128,640]{1,2,0:T(8,128)(2,1)} %copy.38) | copy-start | bytes 5898244
  285.4 28.3 %copy-start.5 = (bf16[12,128,640]{2,1,0:T(8,128)(2,1)S(1)}, bf16[12,128,640]{2,1,0:T(8,128)(2,1)}, u32[]{:S(2)}) copy-start(bf16[12,128,640]{2,1,0:T(8,128)(2,1)} %copy-done.4) | copy-start | bytes 5898244
  313.7 5.5 copy-start.30
  313.7 5.5 copy-start.31
  313.7 5.5 copy-start.41
  324.4 6.4 copy-start.8
  337.4 18.4 %copy-start.36 = (f32[640]{0:T(1024)S(1)}, f32[640]{0:T(1024)}, u32[]{:S(2)}) copy-start(f32[640]{0:T(1024)} %get-tuple-element.20) | copy-start | bytes 7684
  355.8 43.5 %copy-start.26 = (f32[640]{0:T(1024)S(1)}, f32[640]{0:T(1024)}, u32[]{:S(2)}) copy-start(f32[640]{0:T(1024)} %get-tuple-element.14) | copy-start | bytes 7684
  355.8 43.5 %copy-start.27 = (f32[640]{0:T(1024)S(1)}, f32[640]{0:T(1024)}, u32[]{:S(2)}) copy-start(f32[640]{0:T(1024)} %get-tuple-element.59) | copy-start | bytes 7684
  644.8 28.1 %copy-start.7 = (bf16[12,128,640]{2,1,0:T(8,128)(2,1)S(1)}, bf16[12,128,640]{2,1,0:T(8,128)(2,1)}, u32[]{:S(2)}) copy-start(bf16[12,128,640]{2,1,0:T(8,128)(2,1)} %copy-done.6) | copy-start | bytes 5898244
  644.8 28.1 %copy-start.35 = (f32[640]{0:T(1024)S(1)}, f32[640]{0:T(1024)}, u32[]{:S(2)}) copy-start(f32[640]{0:T(1024)} %get-tuple-element.23) | copy-start | bytes 7684
  672.9 5.5 copy-start.24
  672.9 5.5 copy-start.25
  672.9 5.5 copy-start.42
  683.4 6.4 copy-start.9
  696.4 18.4 %copy-start.33 = (f32[640]{0:T(1024)S(1)}, f32[640]{0:T(1024)}, u32[]{:S(2)}) copy-start(f32[640]{0:T(1024)} %get-tuple-element.19) | copy-start | bytes 7684
  714.8 41.9 %copy-start.3 = (bf16[12,8,16,640]{3,2,1,0:T(8,128)(2,1)S(1)}, bf16[12,8,16,640]{3,2,1,0:T(8,128)(2,1)}, u32[]{:S(2)}) copy-start(bf16[12,8,16,640]{3,2,1,0:T(8,128)(2,1)} %param.20) | copy-start | bytes 5898244
  714.8 41.9 %copy-start.32 = (f32[640]{0:T(1024)S(1)}, f32[640]{0:T(1024)}, u32[]{:S(2)}) copy-start(f32[640]{0:T(1024)} %convert_element_type.362) | copy-start | bytes 7684
  714.8 41.9 %copy-start.45 = (bf16[640,640]{1,0:T(8,128)(2,1)S(1)}, bf16[640,640]{1,0:T(8,128)(2,1)}, u32[]{:S(2)}) copy-start(bf16[640,640]{1,0:T(8,128)(2,1)} %param.38) | copy-start | bytes 2457604
  714.8 45.2 %copy-start.1 = (bf16[640,640]{1,0:T(8,128)(2,1)S(1)}, bf16[640,640]{1,0:T(8,128)(2,1)}, u32[]{:S(2)}) copy-start(bf16[640,640]{1,0:T(8,128)(2,1)} %param.24) | copy-start | bytes 2457604
  (16 other events, 46.9 us)
Sparse Core Ops, SparseCore 0:
  45.3 146.3 all-gather.2
  406.1 144.6 all-gather.4
where the time goes:
time: 775 us; the launch traced here: 767 us
  matrix products  321 us (41%)
  waiting for transfers between devices  245 us (32%)
  local copies, waits for them, and re-layouts  151 us (19%)
  blocking collectives  24 us (3%)
  between operations  14.3 us (2%)
  other arithmetic  11.7 us (2%)
    all_gather x2, waiting for transfers between devices, local_forward(): kv_all = lax.all_gather(kv_local, 'sp', axis=2, tiled=True)  244 us
    dot_general x14, matrix products, project(): jnp.einsum('btc,cd->btd', act, weight, preferred_element_type=jnp.float32)  154 us
    slice x6, local copies, waits for them, and re-layouts, local_forward(): attn_out = attend(query, kv_all[0], kv_all[1])  127 us
    sub x4, matrix products, attend(): attn_prob = jax.nn.softmax(scores, axis=-1).astype(jnp.bfloat16)  73.8 us
    dot_general x4, matrix products, attend(): jnp.einsum('bhqk,bkhd->bqhd', attn_prob, v_heads, preferred_element_type=...  63.1 us
    psum x1, blocking collectives, local_forward(): full_sums = lax.psum(part_sums, 'sp')  24 us
    dot_general x2, matrix products, local_forward(): jnp.einsum('blc,jcd->jbld', context, w_cross_kv[layer_idx], preferred_ele...  17.2 us
  transfers between devices with their start and end apart: 2, of which 2 were waited for; matrix products, arithmetic and copies ran while one was open for 6% of the time, Pallas kernels for 0%

commit v1 on v0

v1 whole, which is shorter than its diff:
```python
import functools
import math

import jax
import jax.numpy as jnp
from jax import lax
from jax.experimental import pallas as pl
from jax.experimental.pallas import tpu as pltpu
from jax.sharding import PartitionSpec as P

HEAD_DIM = 64
NUM_GROUPS = 32
CORES = 2
TILE = 256
FF_CHUNK = 512
TEXT_PAD = 128
KEY_CHUNK = 256
LANES = 128
MESH = pl.DeviceIdType.MESH
F32 = jnp.float32
BF16 = jnp.bfloat16
ANY = pl.BlockSpec(memory_space=pl.ANY)
VMEM = pl.BlockSpec(memory_space=pltpu.VMEM)
NT = (((1,), (1,)), ((), ()))


def dot(a, b):
    return jnp.dot(a, b, preferred_element_type=F32)


def dot_nt(a, b):
    return lax.dot_general(a, b, NT, preferred_element_type=F32)


def layer_norm(hidden, gain, bias):
    vals = hidden.astype(F32)
    mean_val = jnp.mean(vals, axis=-1, keepdims=True)
    centered = vals - mean_val
    var_val = jnp.mean(centered * centered, axis=-1, keepdims=True)
    scaled = centered * lax.rsqrt(var_val + 1e-5)
    return (scaled * gain.astype(F32) + bias.astype(F32)).astype(BF16)


def entry_barrier(n):
    me = lax.axis_index('sp')
    sem = pltpu.get_barrier_semaphore()
    for k in range(1, n):
        pl.semaphore_signal(sem, inc=1, device_id={'sp': lax.rem(me + k, n)}, device_id_type=MESH)
    pl.semaphore_wait(sem, n - 1)


def group_sum(row, ind):
    hi = row.astype(BF16)
    rest = row - hi.astype(F32)
    mid = rest.astype(BF16)
    low = (rest - mid.astype(F32)).astype(BF16)
    total = None
    for piece in (low, mid, hi):
        term = dot(jnp.broadcast_to(piece, (16, piece.shape[1])), ind)[0:1]
        total = term if total is None else total + term
    return total


def same_group(ch, group_ch):
    def gid(axis):
        pos = lax.broadcasted_iota(jnp.int32, (ch, ch), axis).astype(F32)
        return jnp.floor((pos + 0.5) * (1.0 / group_ch))
    return jnp.where(gid(0) == gid(1), 1.0, 0.0).astype(BF16)


def column_stats(x_ref, lo, hi, count, ind):
    steps = (hi - lo) // TILE
    zero = jnp.zeros((1, x_ref.shape[1]), F32)

    def rows(i):
        return x_ref[pl.ds(pl.multiple_of(lo + i * TILE, TILE), TILE), :].astype(F32)

    mean = group_sum(lax.fori_loop(0, steps, lambda i, acc: acc + jnp.sum(rows(i), axis=0, keepdims=True), zero), ind) / count

    def sq(i, acc):
        d = rows(i) - mean
        return acc + jnp.sum(d * d, axis=0, keepdims=True)
    return mean, group_sum(lax.fori_loop(0, steps, sq, zero), ind)


def qkv_tile(hid, gain, bias, wqkv, slot, r0, k0, q_ref, k_ref, vt_ref):
    ch = hid.shape[1]
    a = layer_norm(hid, gain, bias)
    r = dot(a, wqkv[...]).astype(BF16)
    q_ref[pl.ds(r0, TILE), :] = r[:, :ch]
    k_ref[slot, pl.ds(k0, TILE), :] = r[:, ch:2 * ch]
    vt_ref[slot, :, pl.ds(k0, TILE)] = r[:, 2 * ch:].T


def head_mask(qp, half):
    lane = lax.broadcasted_iota(jnp.int32, qp.shape, 1)
    return jnp.where((lane >= HEAD_DIM) if half else (lane < HEAD_DIM), qp, jnp.zeros_like(qp))


def self_attend(slot, r0, q_ref, k_ref, vt_ref, s0, s1, ot, scale):
    keys, ch = k_ref.shape[1:]
    pairs = ch // LANES

    def step(cur, top, d0, nxt, pair, half):
        col = pl.multiple_of(pair * LANES, LANES)
        if nxt is not None:
            qm = head_mask(q_ref[pl.ds(r0, TILE), pl.ds(col, LANES)], half)
        new_top = total = acc = None
        for c in range(0, keys, KEY_CHUNK):
            rows = slice(c, c + KEY_CHUNK)
            if nxt is not None:
                s = dot_nt(k_ref[slot, rows, pl.ds(col, LANES)], qm)
                nxt[rows, :] = s
                peak = jnp.max(s, axis=0, keepdims=True)
                new_top = peak if new_top is None else jnp.maximum(new_top, peak)
            if cur is not None:
                p = jnp.exp2(cur[rows, :] * scale - top)
                part = jnp.sum(p, axis=0, keepdims=True)
                prod = dot(vt_ref[slot, pl.ds(d0, HEAD_DIM), rows], p.astype(BF16))
                total = part if total is None else total + part
                acc = prod if acc is None else acc + prod
        if cur is not None:
            ot[pl.ds(d0, HEAD_DIM), :] = (acc / total).astype(BF16)
        return None if nxt is None else new_top * scale

    def body(pair, top):
        d0 = pl.multiple_of(pair * LANES, LANES)
        top = step(s0, top, d0, s1, pair, 1)
        return step(s1, top, pl.multiple_of(d0 + HEAD_DIM, HEAD_DIM), s0, lax.rem(pair + 1, pairs), 0)

    lax.fori_loop(0, pairs, body, step(None, None, 0, s0, 0, 0))


def text_attend(layer, slot, qc, tk, tvt, ot, text_len, scale):
    ch = qc.shape[1]
    used = -(-text_len // 16) * 16
    heads = ch // HEAD_DIM
    scores = []
    for h in range(heads):
        cols = slice(h // 2 * LANES, (h // 2 + 1) * LANES)
        scores.append(dot_nt(tk[layer, slot, 0:used, cols], head_mask(qc[:, cols], h % 2)))
    keep = lax.broadcasted_iota(jnp.int32, scores[0].shape, 0) < text_len
    for h in range(heads):
        s = jnp.where(keep, scores[h], jnp.finfo(F32).min)
        top = jnp.max(s, axis=0, keepdims=True) * scale
        p = jnp.where(keep, jnp.exp2(s * scale - top), 0.0)
        total = jnp.sum(p, axis=0, keepdims=True)
        pb = jnp.concatenate([p.astype(BF16), jnp.zeros((TEXT_PAD - used, p.shape[1]), BF16)], axis=0)
        ot[h * HEAD_DIM:(h + 1) * HEAD_DIM, :] = (dot(tvt[layer, slot, h * HEAD_DIM:(h + 1) * HEAD_DIM, :], pb) / total).astype(BF16)


def whole_kernel(n, per_chip, group_ch,
                 gng_ref, gnb_ref, bin_ref, lng_ref, lnb_ref, bself_ref, bcross_ref, bff1_ref, bff2_ref, bout_ref,
                 x_ref, ctx_ref, win_ref, wself_ref, wcq_ref, wxkv_ref, wco_ref, wff1_ref, wff2_ref, wout_ref,
                 out_ref,
                 xs, hs, qs, k0, k1, vt0, vt1, s0, s1, ot, tk, tvt, vtmp, ctx, wx, win, wout, wo, wcq, wco, wff1, wff2, wqkv,
                 st_mine, st_peer, in_send, in_recv, out_send, out_recv, local_sem, st_sem, kv_send, kv_recv, w_sem, c_sem, x_sem):
    me = lax.axis_index('sp')
    chip, core = me // CORES, lax.rem(me, CORES)
    peer = chip * CORES + (CORES - 1 - core)
    blk, ch = x_ref.shape[1:]
    part = blk // CORES
    own = n * blk
    rows = xs.shape[0]
    shared = rows - own
    ff = wff2.shape[0]
    text_len = ctx_ref.shape[1]
    own_tiles, sh_tiles = own // TILE, shared // TILE
    scale = HEAD_DIM ** -0.5 * math.log2(math.e)
    ks, vts = (k0, k1), (vt0, vt1)
    layers = wself_ref.shape[0]

    ctx_loads = [pltpu.make_async_copy(ctx_ref.at[chip * per_chip + core], ctx.at[0], c_sem.at[0]),
                 pltpu.make_async_copy(ctx_ref.at[chip * per_chip + CORES], ctx.at[1], c_sem.at[1])]

    def text_loads(layer):
        return [pltpu.make_async_copy(wxkv_ref.at[layer, j], wx.at[j], x_sem.at[j]) for j in range(2)]

    def qkv_loads(layer):
        return [pltpu.make_async_copy(wself_ref.at[layer, j], wqkv.at[:, pl.ds(j * ch, ch)], w_sem.at[j]) for j in range(3)]

    def layer_loads(layer):
        pairs = ((wself_ref.at[layer, 3], wo), (wcq_ref.at[layer], wcq), (wco_ref.at[layer], wco), (wff1_ref.at[layer], wff1), (wff2_ref.at[layer], wff2))
        return [pltpu.make_async_copy(src, dst, w_sem.at[3 + j]) for j, (src, dst) in enumerate(pairs)]

    edge_loads = [pltpu.make_async_copy(win_ref, win, w_sem.at[8]), pltpu.make_async_copy(wout_ref, wout, w_sem.at[9])]

    def begin(copies):
        for c in copies:
            c.start()

    def finish(copies):
        for c in copies:
            c.wait()

    def in_copy(i, src, dest):
        to_chip, to_core = dest // CORES, lax.rem(dest, CORES)
        source = (x_ref.at[to_chip * per_chip + to_core],
                  x_ref.at[to_chip * per_chip + CORES, pl.ds(pl.multiple_of(to_core * part, part), part)])[i]
        target = (xs.at[pl.ds(pl.multiple_of(src * blk, blk), blk)],
                  xs.at[pl.ds(pl.multiple_of(own + src * part, part), part)])[i]
        return source, target

    def in_remote(i, src, dest):
        source, target = in_copy(i, src, dest)
        return pltpu.make_async_remote_copy(
            src_ref=source, dst_ref=target, send_sem=in_send.at[i, dest], recv_sem=in_recv.at[i, src],
            device_id={'sp': dest}, device_id_type=MESH)

    def out_copy(i, src, dest):
        from_chip, from_core = src // CORES, lax.rem(src, CORES)
        source = (xs.at[pl.ds(pl.multiple_of(dest * blk, blk), blk)],
                  xs.at[pl.ds(pl.multiple_of(own + dest * part, part), part)])[i]
        target = (out_ref.at[from_chip * per_chip + from_core],
                  out_ref.at[from_chip * per_chip + CORES, pl.ds(pl.multiple_of(from_core * part, part), part)])[i]
        return source, target

    def out_remote(i, src, dest):
        source, target = out_copy(i, src, dest)
        return pltpu.make_async_remote_copy(
            src_ref=source, dst_ref=target, send_sem=out_send.at[i, dest], recv_sem=out_recv.at[i, src],
            device_id={'sp': dest}, device_id_type=MESH)

    def out_local(i):
        source, target = out_copy(i, me, me)
        return pltpu.make_async_copy(source, target, local_sem.at[2 + i])

    def send_out(i, dest):
        @pl.when(dest != me)
        def _():
            out_remote(i, me, dest).start()

        @pl.when(dest == me)
        def _():
            out_local(i).start()

    def kv_copies(layer):
        k, vt = ks[layer], vts[layer]
        args = ((k.at[1, pl.ds(0, shared)], k.at[1, pl.ds(shared, shared)]),
                (vt.at[1, :, pl.ds(0, shared)], vt.at[1, :, pl.ds(shared, shared)]))
        return [pltpu.make_async_remote_copy(
            src_ref=a, dst_ref=b, send_sem=kv_send.at[layer, j], recv_sem=kv_recv.at[layer, j],
            device_id={'sp': peer}, device_id_type=MESH) for j, (a, b) in enumerate(args)]

    begin(ctx_loads)
    begin(text_loads(0))
    locals_in = [pltpu.make_async_copy(*in_copy(i, me, me), local_sem.at[i]) for i in range(2)]
    begin(locals_in)
    entry_barrier(n)
    for i in (1, 0):
        for k in range(1, n):
            in_remote(i, me, lax.rem(me + k, n)).start()
    begin(edge_loads)
    begin(qkv_loads(0))

    tk[...] = jnp.zeros_like(tk)
    vtmp[...] = jnp.zeros_like(vtmp)
    finish(ctx_loads)
    for layer in range(layers):
        finish(text_loads(layer))
        for s in range(2):
            tk[layer, s, 0:text_len, :] = dot(ctx[s], wx[0]).astype(BF16)
            vtmp[0:text_len, :] = dot(ctx[s], wx[1]).astype(BF16)
            tvt[layer, s] = vtmp[...].T
        if layer + 1 < layers:
            begin(text_loads(layer + 1))
    begin(layer_loads(0))
    ind = same_group(ch, group_ch)

    locals_in[1].wait()
    for k in range(1, n):
        in_remote(1, lax.rem(me + k, n), me).wait_recv()
    half = float(shared * group_ch)
    mean, m2 = column_stats(xs, own, rows, half, ind)
    st_mine[...] = jnp.zeros_like(st_mine)
    st_mine[0:1, :] = mean
    st_mine[1:2, :] = m2
    st_copy = pltpu.make_async_remote_copy(
        src_ref=st_mine, dst_ref=st_peer, send_sem=st_sem.at[0], recv_sem=st_sem.at[1], device_id={'sp': peer}, device_id_type=MESH)
    st_copy.start()
    finish(edge_loads)
    finish(qkv_loads(0))
    st_copy.wait()
    delta = mean - st_peer[0:1, :]
    mean_sh = (mean + st_peer[0:1, :]) * 0.5
    m2 = m2 + st_peer[1:2, :] + delta * delta * (half * 0.5)
    inv_sh = lax.rsqrt(m2 / (2.0 * half) + 1e-6)
    gain = gng_ref[...].astype(F32)
    off = gnb_ref[...].astype(F32)

    def enter(slot, mean, inv):
        def tile(i, carry):
            r0 = pl.multiple_of(slot * own + i * TILE, TILE)
            x = xs[pl.ds(r0, TILE), :].astype(F32)
            g = ((x - mean) * inv * gain + off).astype(BF16)
            hid = (dot(g, win[...]) + bin_ref[...].astype(F32)).astype(BF16)
            hs[pl.ds(r0, TILE), :] = hid
            qkv_tile(hid, lng_ref[0, 0:1, :], lnb_ref[0, 0:1, :], wqkv, slot, r0, pl.multiple_of(i * TILE, TILE), qs, k0, vt0)
            return carry
        return tile
    lax.fori_loop(0, sh_tiles, enter(1, mean_sh, inv_sh), 0)
    begin(kv_copies(0))

    locals_in[0].wait()
    for k in range(1, n):
        in_remote(0, lax.rem(me + k, n), me).wait_recv()
    count = float(own * group_ch)
    mean, m2 = column_stats(xs, 0, own, count, ind)
    lax.fori_loop(0, own_tiles, enter(0, mean, lax.rsqrt(m2 / count + 1e-6)), 0)

    for layer in range(layers):
        last = layer == layers - 1
        k_all, vt_all = ks[layer], vts[layer]
        loads = layer_loads(layer)
        if layer:
            begin(loads)
        if not last:
            begin(qkv_loads(layer + 1))
        for c in kv_copies(layer):
            c.wait_recv()

        def tile(it, carry):
            f = (it + own_tiles - sh_tiles) // own_tiles
            slot = 1 - f
            idx = f * lax.rem(chip + 1 + it + own_tiles - sh_tiles, own_tiles) + slot * (own_tiles + it)
            r0 = pl.multiple_of(idx * TILE, TILE)
            k0r = pl.multiple_of(idx * TILE - slot * own, TILE)
            self_attend(slot, r0, qs, k_all, vt_all, s0, s1, ot, scale)

            @pl.when(it == 0)
            def _():
                finish(loads)
                if not last:
                    finish(qkv_loads(layer + 1))
            hid = (hs[pl.ds(r0, TILE), :].astype(F32) + dot(ot[...].T, wo[...]) + bself_ref[layer:layer + 1, :].astype(F32)).astype(BF16)
            qc = dot(layer_norm(hid, lng_ref[1, layer:layer + 1, :], lnb_ref[1, layer:layer + 1, :]), wcq[...]).astype(BF16)
            text_attend(layer, slot, qc, tk, tvt, ot, text_len, scale)
            hid = (hid.astype(F32) + dot(ot[...].T, wco[...]) + bcross_ref[layer:layer + 1, :].astype(F32)).astype(BF16)
            a = layer_norm(hid, lng_ref[2, layer:layer + 1, :], lnb_ref[2, layer:layer + 1, :])
            acc = None
            for c0 in range(0, ff, FF_CHUNK):
                pc, qcol = slice(c0, c0 + FF_CHUNK), slice(ff + c0, ff + c0 + FF_CHUNK)
                p = (dot(a, wff1[:, pc]) + bff1_ref[layer:layer + 1, pc].astype(F32)).astype(BF16).astype(F32)
                g = (dot(a, wff1[:, qcol]) + bff1_ref[layer:layer + 1, qcol].astype(F32)).astype(BF16).astype(F32)
                z = (p * (0.5 * g * (1.0 + lax.erf(g * math.sqrt(0.5))))).astype(BF16)
                prod = dot(z, wff2[pc, :])
                acc = prod if acc is None else acc + prod
            hid = (hid.astype(F32) + acc + bff2_ref[layer:layer + 1, :].astype(F32)).astype(BF16)
            if last:
                y = dot(hid, wout[...]) + bout_ref[...].astype(F32) + xs[pl.ds(r0, TILE), :].astype(F32)
                xs[pl.ds(r0, TILE), :] = y.astype(BF16)

                @pl.when(slot == 0)
                def _():
                    for j in range(TILE // blk):
                        send_out(0, idx * (TILE // blk) + j)

                @pl.when(slot == 1)
                def _():
                    for j in range(TILE // part):
                        send_out(1, (idx - own_tiles) * (TILE // part) + j)
            else:
                hs[pl.ds(r0, TILE), :] = hid
                qkv_tile(hid, lng_ref[0, layer + 1:layer + 2, :], lnb_ref[0, layer + 1:layer + 2, :], wqkv, slot, r0, k0r, qs,
                         ks[layer + 1], vts[layer + 1])

                @pl.when(it == sh_tiles - 1)
                def _():
                    begin(kv_copies(layer + 1))
            return carry
        lax.fori_loop(0, own_tiles + sh_tiles, tile, 0)

    for layer in range(layers):
        for c in kv_copies(layer):
            c.wait_send()
    for i in range(2):
        out_local(i).wait()
        for k in range(1, n):
            other = lax.rem(me + k, n)
            in_remote(i, me, other).wait_send()
            out_remote(i, me, other).wait_send()
            out_remote(i, other, me).wait_recv()


def solution(mesh):
    n = mesh.shape['sp']
    tok_spec = P('dp', 'sp', None, None)
    ctx_spec = P('dp', None, None)
    replicated = P()
    dma = pltpu.SemaphoreType.DMA

    def local_forward(latent, context, gn_gain, gn_bias, w_in, b_in, ln_gain, ln_bias, w_self, b_self, w_cross_q, w_cross_kv, w_cross_o, b_cross, w_ff1, b_ff1, w_ff2, b_ff2, w_out, b_out):
        batch, rows, columns, ch = latent.shape
        blk = rows * columns
        ff = w_ff2.shape[1]
        layers, text_len, text_dim = w_self.shape[0], context.shape[1], context.shape[2]
        per_chip = batch * CORES // n
        assert per_chip == CORES + 1 and layers == 2
        own = n * blk
        toks = own + own // CORES

        def vm(*dims, dtype=BF16):
            return pltpu.VMEM(dims, dtype)

        scratch = [
            vm(toks, ch), vm(toks, ch), vm(toks, ch), vm(2, own, ch), vm(2, own, ch), vm(2, ch, own), vm(2, ch, own),
            vm(own, TILE, dtype=F32), vm(own, TILE, dtype=F32), vm(ch, TILE),
            vm(layers, 2, TEXT_PAD, ch), vm(layers, 2, ch, TEXT_PAD), vm(TEXT_PAD, ch), vm(2, text_len, text_dim), vm(2, text_dim, ch),
            vm(ch, ch), vm(ch, ch), vm(ch, ch), vm(ch, ch), vm(ch, ch), vm(ch, 2 * ff), vm(ff, ch), vm(ch, 3 * ch),
            vm(8, ch, dtype=F32), vm(8, ch, dtype=F32),
            dma((2, n)), dma((2, n)), dma((2, n)), dma((2, n)), dma((4,)), dma((2,)), dma((layers, 2)), dma((layers, 2)), dma((10,)), dma((2,)), dma((2,))]
        small = [gn_gain[None], gn_bias[None], b_in[None], ln_gain.transpose(1, 0, 2), ln_bias.transpose(1, 0, 2), b_self, b_cross, b_ff1, b_ff2, b_out[None]]
        big = [latent.reshape(batch, blk, ch), context, w_in, w_self, w_cross_q, w_cross_kv, w_cross_o, w_ff1, w_ff2, w_out]
        out = pl.pallas_call(
            functools.partial(whole_kernel, n, per_chip, ch // NUM_GROUPS),
            out_shape=jax.ShapeDtypeStruct((batch, blk, ch), BF16),
            in_specs=[VMEM] * len(small) + [ANY] * len(big), out_specs=ANY, scratch_shapes=scratch,
            compiler_params=pltpu.CompilerParams(collective_id=0, has_side_effects=True, vmem_limit_bytes=62 * 1024 * 1024),
        )(*small, *big)
        return out.reshape(batch, rows, columns, ch)

    in_specs = (tok_spec, ctx_spec) + (replicated,) * 18
    return jax.shard_map(local_forward, mesh=mesh, in_specs=in_specs, out_specs=tok_spec, check_vma=False)
```

time: 775 us -> 180 us (0.23)
  matrix products: 321 us -> 0 us
  waiting for transfers between devices: 245 us -> 0 us
  Pallas kernels: 0 us -> 172 us
  local copies, waits for them, and re-layouts: 151 us -> 8.07 us
  blocking collectives: 24 us -> 0 us
  between operations: 14.3 us -> 0.01 us
  other arithmetic: 11.7 us -> 0 us
    dot_general x22 -> x0, matrix products: 247 us -> none  [the longest x14 154 us: project(): jnp.einsum('btc,cd->btd', act, weight, preferred_element_type=jnp.float32)]
    all_gather x2 -> x0, waiting for transfers between devices: 244 us -> none  [local_forward(): kv_all = lax.all_gather(kv_local, 'sp', axis=2, tiled=True)]
    pallas_call x0 -> x1, Pallas kernels: none -> 172 us  [local_forward(): pl.pallas_call(functools.partial(whole_kernel, n, per_chip, ch // NUM_GRO...]
    slice x12 -> x0, local copies, waits for them, and re-layouts: 136 us -> none  [the longest x6 127 us: local_forward(): attn_out = attend(query, kv_all[0], kv_all[1])]
    sub x4 -> x0, matrix products: 73.8 us -> none  [attend(): attn_prob = jax.nn.softmax(scores, axis=-1).astype(jnp.bfloat16)]
    psum x1 -> x0, blocking collectives: 24 us -> none  [local_forward(): full_sums = lax.psum(part_sums, 'sp')]
    convert_element_type x4 -> x0, local copies, waits for them, and re-layouts: 12 us -> none  [the longest x2 6.77 us: local_forward(): query = project(normed, w_self[layer_idx, 0]).astype(jnp.bfloat16)]
  transfers between devices with their start and end apart: 2 -> 0, of which waited for: 2 -> 0; matrix products, arithmetic and copies ran while one was open for 6% -> 0% of each run, Pallas kernels for 0% -> 0%
where the time goes in v1:
time: 180 us
  Pallas kernels  172 us (96%)
  local copies, waits for them, and re-layouts  8.07 us (4%)
    pallas_call x1, Pallas kernels, local_forward(): pl.pallas_call(functools.partial(whole_kernel, n, per_chip, ch // NUM_GRO...  172 us

profile of v1, /device:TPU:113, one launch (start us, length us, event | category | flops | bytes accessed | tf_op | source)
XLA Modules:
  0.0 179.7 jit_solution(8154838430737370422)
XLA Ops:
  0.0 1.3 broadcast_in_dim.12.gng_ref
  1.3 1.3 broadcast_in_dim.13.gnb_ref
  2.5 1.3 broadcast_in_dim.14.bin_ref
  3.8 1.3 broadcast_in_dim.15.bout_ref
  5.1 171.7 %shard_map.190 = bf16[12,128,640]{2,1,0:T(8,128)(2,1)} custom-call(bf16[1,640]{1,0:T(2,128)(2,1)} %broadcast_in_dim.12.gng_ref, bf16[1,640]{1,0:T(2,128)(2,1)} %broadcast_in_dim.13.gnb_ref, bf16[1,640]{1,0:T(2,128)(2,1)} %broadcast_in_dim.14.bin_ref, bf16[3,2,640]{2,1,0:T(2,128)(2,1)} %bitcast.6, bf16[3,2,640]{2,1,0:T(2,128)(2,1)} %bitcast.7, ...), custom_call_target="tpu_custom_call" | custom-call | tf_op jit(solution)/shard_map/pallas_call | solution.py:414
  176.7 3.0 %copy.22 = bf16[12,8,16,640]{3,2,1,0:T(8,128)(2,1)} copy(bf16[12,8,16,640]{3,2,1,0:T(8,128)(2,1)} %bitcast.4) | data formatting | bytes 3932160

commit v2 on v1

--- a/solution.py
+++ b/solution.py
@@ -153,7 +153,7 @@
                  gng_ref, gnb_ref, bin_ref, lng_ref, lnb_ref, bself_ref, bcross_ref, bff1_ref, bff2_ref, bout_ref,
                  x_ref, ctx_ref, win_ref, wself_ref, wcq_ref, wxkv_ref, wco_ref, wff1_ref, wff2_ref, wout_ref,
                  out_ref,
-                 xs, hs, qs, k0, k1, vt0, vt1, s0, s1, ot, tk, tvt, vtmp, ctx, wx, win, wout, wo, wcq, wco, wff1, wff2, wqkv,
+                 xs, hs, qs, k0, k1, vt0, vt1, s0, s1, ot, tk, tvt, vtmp, ctx, wx, win, wout, wo, wcq, wco, wff1, wff2, wqkv0, wqkv1,
                  st_mine, st_peer, in_send, in_recv, out_send, out_recv, local_sem, st_sem, kv_send, kv_recv, w_sem, c_sem, x_sem):
     me = lax.axis_index('sp')
     chip, core = me // CORES, lax.rem(me, CORES)
@@ -167,7 +167,7 @@
     text_len = ctx_ref.shape[1]
     own_tiles, sh_tiles = own // TILE, shared // TILE
     scale = HEAD_DIM ** -0.5 * math.log2(math.e)
-    ks, vts = (k0, k1), (vt0, vt1)
+    ks, vts, wqkvs = (k0, k1), (vt0, vt1), (wqkv0, wqkv1)
     layers = wself_ref.shape[0]
 
     ctx_loads = [pltpu.make_async_copy(ctx_ref.at[chip * per_chip + core], ctx.at[0], c_sem.at[0]),
@@ -177,7 +177,7 @@
         return [pltpu.make_async_copy(wxkv_ref.at[layer, j], wx.at[j], x_sem.at[j]) for j in range(2)]
 
     def qkv_loads(layer):
-        return [pltpu.make_async_copy(wself_ref.at[layer, j], wqkv.at[:, pl.ds(j * ch, ch)], w_sem.at[j]) for j in range(3)]
+        return [pltpu.make_async_copy(wself_ref.at[layer, j], wqkvs[layer].at[:, pl.ds(j * ch, ch)], w_sem.at[10 * layer + j]) for j in range(3)]
 
     def layer_loads(layer):
         pairs = ((wself_ref.at[layer, 3], wo), (wcq_ref.at[layer], wcq), (wco_ref.at[layer], wco), (wff1_ref.at[layer], wff1), (wff2_ref.at[layer], wff2))
@@ -265,6 +265,7 @@
         if layer + 1 < layers:
             begin(text_loads(layer + 1))
     begin(layer_loads(0))
+    begin(qkv_loads(1))
     ind = same_group(ch, group_ch)
 
     locals_in[1].wait()
@@ -285,28 +286,29 @@
     mean_sh = (mean + st_peer[0:1, :]) * 0.5
     m2 = m2 + st_peer[1:2, :] + delta * delta * (half * 0.5)
     inv_sh = lax.rsqrt(m2 / (2.0 * half) + 1e-6)
-    gain = gng_ref[...].astype(F32)
-    off = gnb_ref[...].astype(F32)
+    gain = gng_ref[...].astype(F32)[None, :]
+    off = gnb_ref[...].astype(F32)[None, :]
 
     def enter(slot, mean, inv):
         def tile(i, carry):
             r0 = pl.multiple_of(slot * own + i * TILE, TILE)
             x = xs[pl.ds(r0, TILE), :].astype(F32)
             g = ((x - mean) * inv * gain + off).astype(BF16)
-            hid = (dot(g, win[...]) + bin_ref[...].astype(F32)).astype(BF16)
+            hid = (dot(g, win[...]) + bin_ref[...].astype(F32)[None, :]).astype(BF16)
             hs[pl.ds(r0, TILE), :] = hid
-            qkv_tile(hid, lng_ref[0, 0:1, :], lnb_ref[0, 0:1, :], wqkv, slot, r0, pl.multiple_of(i * TILE, TILE), qs, k0, vt0)
+            qkv_tile(hid, lng_ref[0, 0:1, :], lnb_ref[0, 0:1, :], wqkv0, slot, r0, pl.multiple_of(i * TILE, TILE), qs, k0, vt0)
             return carry
         return tile
     lax.fori_loop(0, sh_tiles, enter(1, mean_sh, inv_sh), 0)
     begin(kv_copies(0))
 
-    locals_in[0].wait()
-    for k in range(1, n):
-        in_remote(0, lax.rem(me + k, n), me).wait_recv()
-    count = float(own * group_ch)
-    mean, m2 = column_stats(xs, 0, own, count, ind)
-    lax.fori_loop(0, own_tiles, enter(0, mean, lax.rsqrt(m2 / count + 1e-6)), 0)
+    def own_entry():
+        locals_in[0].wait()
+        for k in range(1, n):
+            in_remote(0, lax.rem(me + k, n), me).wait_recv()
+        count = float(own * group_ch)
+        mean, m2 = column_stats(xs, 0, own, count, ind)
+        lax.fori_loop(0, own_tiles, enter(0, mean, lax.rsqrt(m2 / count + 1e-6)), 0)
 
     for layer in range(layers):
         last = layer == layers - 1
@@ -314,8 +316,6 @@
         loads = layer_loads(layer)
         if layer:
             begin(loads)
-        if not last:
-            begin(qkv_loads(layer + 1))
         for c in kv_copies(layer):
             c.wait_recv()
 
@@ -325,6 +325,8 @@
             idx = f * lax.rem(chip + 1 + it + own_tiles - sh_tiles, own_tiles) + slot * (own_tiles + it)
             r0 = pl.multiple_of(idx * TILE, TILE)
             k0r = pl.multiple_of(idx * TILE - slot * own, TILE)
+            if layer == 0:
+                pl.when(it == sh_tiles)(own_entry)
             self_attend(slot, r0, qs, k_all, vt_all, s0, s1, ot, scale)
 
             @pl.when(it == 0)
@@ -347,7 +349,7 @@
                 acc = prod if acc is None else acc + prod
             hid = (hid.astype(F32) + acc + bff2_ref[layer:layer + 1, :].astype(F32)).astype(BF16)
             if last:
-                y = dot(hid, wout[...]) + bout_ref[...].astype(F32) + xs[pl.ds(r0, TILE), :].astype(F32)
+                y = dot(hid, wout[...]) + bout_ref[...].astype(F32)[None, :] + xs[pl.ds(r0, TILE), :].astype(F32)
                 xs[pl.ds(r0, TILE), :] = y.astype(BF16)
 
                 @pl.when(slot == 0)
@@ -361,7 +363,7 @@
                         send_out(1, (idx - own_tiles) * (TILE // part) + j)
             else:
                 hs[pl.ds(r0, TILE), :] = hid
-                qkv_tile(hid, lng_ref[0, layer + 1:layer + 2, :], lnb_ref[0, layer + 1:layer + 2, :], wqkv, slot, r0, k0r, qs,
+                qkv_tile(hid, lng_ref[0, layer + 1:layer + 2, :], lnb_ref[0, layer + 1:layer + 2, :], wqkvs[layer + 1], slot, r0, k0r, qs,
                          ks[layer + 1], vts[layer + 1])
 
                 @pl.when(it == sh_tiles - 1)
@@ -406,10 +408,10 @@
             vm(toks, ch), vm(toks, ch), vm(toks, ch), vm(2, own, ch), vm(2, own, ch), vm(2, ch, own), vm(2, ch, own),
             vm(own, TILE, dtype=F32), vm(own, TILE, dtype=F32), vm(ch, TILE),
             vm(layers, 2, TEXT_PAD, ch), vm(layers, 2, ch, TEXT_PAD), vm(TEXT_PAD, ch), vm(2, text_len, text_dim), vm(2, text_dim, ch),
-            vm(ch, ch), vm(ch, ch), vm(ch, ch), vm(ch, ch), vm(ch, ch), vm(ch, 2 * ff), vm(ff, ch), vm(ch, 3 * ch),
+            vm(ch, ch), vm(ch, ch), vm(ch, ch), vm(ch, ch), vm(ch, ch), vm(ch, 2 * ff), vm(ff, ch), vm(ch, 3 * ch), vm(ch, 3 * ch),
             vm(8, ch, dtype=F32), vm(8, ch, dtype=F32),
-            dma((2, n)), dma((2, n)), dma((2, n)), dma((2, n)), dma((4,)), dma((2,)), dma((layers, 2)), dma((layers, 2)), dma((10,)), dma((2,)), dma((2,))]
-        small = [gn_gain[None], gn_bias[None], b_in[None], ln_gain.transpose(1, 0, 2), ln_bias.transpose(1, 0, 2), b_self, b_cross, b_ff1, b_ff2, b_out[None]]
+            dma((2, n)), dma((2, n)), dma((2, n)), dma((2, n)), dma((4,)), dma((2,)), dma((layers, 2)), dma((layers, 2)), dma((13,)), dma((2,)), dma((2,))]
+        small = [gn_gain, gn_bias, b_in, ln_gain.transpose(1, 0, 2), ln_bias.transpose(1, 0, 2), b_self, b_cross, b_ff1, b_ff2, b_out]
         big = [latent.reshape(batch, blk, ch), context, w_in, w_self, w_cross_q, w_cross_kv, w_cross_o, w_ff1, w_ff2, w_out]
         out = pl.pallas_call(
             functools.partial(whole_kernel, n, per_chip, ch // NUM_GROUPS),

time: 180 us -> 170 us (0.944)
  Pallas kernels: 172 us -> 166 us
  local copies, waits for them, and re-layouts: 8.07 us -> 3.01 us
    pallas_call x1, Pallas kernels: 172 us -> 166 us  [local_forward(): pl.pallas_call(functools.partial(whole_kernel, n, per_chip, ch // NUM_GRO...]
    broadcast_in_dim x4 -> x0, local copies, waits for them, and re-layouts: 5.05 us -> none  [the longest x1 1.27 us: local_forward(): gn_bias[None]]
where the time goes in v2:
time: 170 us; the launch traced here: 169 us
  Pallas kernels  166 us (98%)
  local copies, waits for them, and re-layouts  3.01 us (2%)
    pallas_call x1, Pallas kernels, local_forward(): pl.pallas_call(functools.partial(whole_kernel, n, per_chip, ch // NUM_GRO...  166 us

profile of v2, /device:TPU:113, one launch (start us, length us, event | category | flops | bytes accessed | tf_op | source)
XLA Modules:
  0.0 169.5 jit_solution(7917973684163215740)
XLA Ops:
  0.0 166.4 %shard_map.190 = bf16[12,128,640]{2,1,0:T(8,128)(2,1)} custom-call(bf16[640]{0:T(1024)(128)(2,1)} %gng_ref.1, bf16[640]{0:T(1024)(128)(2,1)} %gnb_ref.1, bf16[640]{0:T(1024)(128)(2,1)} %bin_ref.1, bf16[3,2,640]{2,1,0:T(2,128)(2,1)} %bitcast.6, bf16[3,2,640]{2,1,0:T(2,128)(2,1)} %bitcast.7, bf16[2,640]{1,0:T(2,128)(2,1)} %bself_ref.1, ...), custom_call_target="tpu_custom_call" | custom-call | tf_op jit(solution)/shard_map/pallas_call | solution.py:416
  166.4 3.0 %copy.22 = bf16[12,8,16,640]{3,2,1,0:T(8,128)(2,1)} copy(bf16[12,8,16,640]{3,2,1,0:T(8,128)(2,1)} %bitcast.4) | data formatting | bytes 3932160
